TPU v7x, 256 devices: a whole 4x4x8 slice. The times are simulated.
256 devices in a mesh: pop: 8 (over x_lo, y), dp: 32 (over z, x_hi, core).
Axes of the slice: x: 4 (x_hi: 2, x_lo: 2; x = x_hi * 2 + x_lo), y: 4, z: 8, core: 2. Of those that a mesh axis runs over, the one named last changes fastest.
Arguments:
- observations: bfloat16 [8, 16384, 256], P('pop', 'dp'), may hold values from -6 to 6
- returns: float32 [8, 16384], P('pop', 'dp'), may hold values from 0 to 2
- actions: int32 [8, 16384], P('pop', 'dp'), may hold values from 0 to 17
- w_input: bfloat16 [8, 256, 2048], P('pop', 'dp'), may hold values from -0.375 to 0.375
- w_middle: bfloat16 [8, 2048, 2048], P('pop', 'dp'), may hold values from -0.125 to 0.125
- w_head: bfloat16 [8, 2048, 18], P('pop', 'dp'), may hold values from -0.125 to 0.125
- log_rate: float32 [8], replicated, may hold values from 3 to 4
- copy_from: int32 [8], replicated, may hold values from 0 to 1, as said below
- perturb: int32 [8], replicated, may hold values from 0 to 2
Outputs:
- next_input: bfloat16 [8, 256, 2048], P('pop', 'dp')
- next_middle: bfloat16 [8, 2048, 2048], P('pop', 'dp')
- next_head: bfloat16 [8, 2048, 18], P('pop', 'dp')
- next_log_rate: float32 [8], P('pop')
- fitness: float32 [8], P('pop')
Inputs may be any that keep to these rules, and one draw needn't show every extreme that they name: Some two members that lie 4 apart have copy_from 1.
All inputs are finite; a program needn't handle non-finite values.
Results may differ from a plain program's by a relative error of at most 0.014.
Values may be sent and summed in bfloat16 or wider, within the bound.
A program may use at most 128 MiB of HBM per device.

v0:
```python
import jax
import jax.numpy as jnp
from jax import lax
from jax.sharding import PartitionSpec as P

CAP = 2.0


def joined_along(parts, dim):
    parts = jnp.moveaxis(parts, 0, dim)
    lengths = parts.shape
    return parts.reshape(*lengths[:dim], lengths[dim] * lengths[dim + 1], *lengths[dim + 2 :])


def gather_packed(arrays, axis, dims):
    line = jnp.concatenate([a.reshape(-1) for a in arrays])
    lines, at, done = (lax.all_gather(line, axis), 0, [])
    for a, dim in zip(arrays, dims):
        parts = lines[:, at : at + a.size].reshape(-1, *a.shape)
        done.append(joined_along(parts, dim))
        at += a.size
    return tuple(done)


def from_everyone(shard, axis):
    peers = lax.axis_size(axis)
    return lax.all_to_all(
        jnp.broadcast_to(shard[None], (peers, *shard.shape)), axis, 0, 0, tiled=True
    )


def of_everyone(shard, axis):
    everything = from_everyone(shard, axis)
    return jnp.sum(everything, axis=0)


def in_blocks(shard, dim, peers):
    before, after = (shard.shape[:dim], shard.shape[dim + 1 :])
    return jnp.moveaxis(shard.reshape(*before, peers, -1, *after), dim, 0)


def sum_at_owner(shard, axis, dim):
    peers = lax.axis_size(axis)
    parts = lax.all_to_all(in_blocks(shard, dim, peers), axis, 0, 0, tiled=True)
    return jnp.sum(parts.astype(jnp.float32), axis=0)


def shifted(block, axis, distance):
    devices = range(lax.axis_size(axis))
    route = [((i - distance) % len(devices), i) for i in devices]
    return lax.ppermute(block, axis, route)


def silu_slope(pre):
    sig = jax.nn.sigmoid(pre)
    return sig * (1.0 + pre * (1.0 - sig))


def contract_rows(left, right):
    return lax.dot_general(
        left, right, (((0,), (0,)), ((), ())), preferred_element_type=jnp.float32
    )


def contract_cols(left, right):
    return lax.dot_general(
        left, right, (((1,), (1,)), ((), ())), preferred_element_type=jnp.float32
    )


def local(observations, returns, actions, w_input, w_middle, w_head, log_rate, copy_from, perturb):
    obs = observations[0]
    gains = returns[0]
    chosen = actions[0]
    own_first = w_input[0]
    own_middle = w_middle[0]
    own_head = w_head[0]
    rows = obs.shape[0]
    batch = rows * lax.axis_size("dp")
    first, head = gather_packed((own_first, own_head), "dp", (0, 0))
    pre1 = jnp.dot(obs, first, preferred_element_type=jnp.float32)
    hidden1 = jax.nn.silu(pre1).astype(jnp.bfloat16)
    whole = lax.all_gather(own_middle, "dp", axis=0, tiled=True)
    pre2 = jnp.dot(hidden1, whole, preferred_element_type=jnp.float32)
    hidden2 = jax.nn.silu(pre2).astype(jnp.bfloat16)
    squash = jnp.tanh(jnp.dot(hidden2, head, preferred_element_type=jnp.float32) / CAP)
    logits = CAP * squash
    logp = logits - jnp.log(jnp.sum(jnp.exp(logits), axis=1, keepdims=True))
    onehot = (chosen[:, None] == lax.broadcasted_iota(jnp.int32, logits.shape, 1)).astype(
        jnp.float32
    )
    taken = jnp.sum(logp * onehot, axis=1)
    fitness = of_everyone(jnp.sum(gains * taken) / batch, "dp")
    grad_raw = (
        -(gains / batch)[:, None] * (onehot - jnp.exp(logp)) * (1.0 - squash * squash)
    ).astype(jnp.bfloat16)
    head_term = contract_rows(hidden2, grad_raw)
    grad_pre2 = (contract_cols(grad_raw, head) * silu_slope(pre2)).astype(jnp.bfloat16)
    grad_middle = lax.psum_scatter(
        contract_rows(hidden1, grad_pre2).astype(jnp.bfloat16),
        "dp",
        scatter_dimension=0,
        tiled=True,
    ).astype(jnp.float32)
    member = lax.axis_index("pop")
    members = lax.axis_size("pop")
    rate = jnp.exp(lax.dynamic_index_in_dim(log_rate, member, keepdims=False))
    new_middle = (own_middle.astype(jnp.float32) - rate * grad_middle).astype(jnp.bfloat16)
    back = contract_cols(grad_pre2, whole)
    grad_pre1 = (back * silu_slope(pre1)).astype(jnp.bfloat16)
    input_term = contract_rows(obs, grad_pre1)
    grad_first, grad_head = (
        sum_at_owner(input_term.astype(jnp.bfloat16), "dp", 0),
        sum_at_owner(head_term.astype(jnp.bfloat16), "dp", 0),
    )
    new_first = (own_first.astype(jnp.float32) - rate * grad_first).astype(jnp.bfloat16)
    new_head = (own_head.astype(jnp.float32) - rate * grad_head).astype(jnp.bfloat16)
    moved_first, moved_middle, moved_head = shifted((new_first, new_middle, new_head), "pop", 1)
    flag = lax.dynamic_index_in_dim(copy_from, member, keepdims=False) == 1
    out_first = jnp.where(flag, moved_first, new_first)
    out_middle = jnp.where(flag, moved_middle, new_middle)
    out_head = jnp.where(flag, moved_head, new_head)
    source = jnp.where(flag, (member + members - 1) % members, member)
    pick = lax.dynamic_index_in_dim(perturb, member, keepdims=False)
    offset = jnp.where(pick == 0, -0.2, jnp.where(pick == 1, 0.0, 0.2)).astype(jnp.float32)
    next_rate = lax.dynamic_index_in_dim(log_rate, source, keepdims=False) + offset
    return (
        out_first[None],
        out_middle[None],
        out_head[None],
        next_rate.reshape(1),
        fitness.reshape(1),
    )


def solution(mesh):
    in_specs = (
        P("pop", "dp", None),
        P("pop", "dp"),
        P("pop", "dp"),
        P("pop", "dp", None),
        P("pop", "dp", None),
        P("pop", "dp", None),
        P(),
        P(),
        P(),
    )
    out_specs = (
        P("pop", "dp", None),
        P("pop", "dp", None),
        P("pop", "dp", None),
        P("pop"),
        P("pop"),
    )
    return jax.shard_map(local, mesh=mesh, in_specs=in_specs, out_specs=out_specs, check_vma=False)
```

profile of v0, /device:TPU:2, one launch (start us, length us, event | category | flops | bytes accessed | tf_op | source)
XLA Modules:
  0.0 389.5 jit_solution(15649825401868657893)
XLA Ops:
  7.2 0.8 copy.37
  8.1 0.1 reshape_squeeze.7
  8.2 0.8 copy.50
  9.0 0.7 reshape.61
  9.7 0.0 all-gather.6.cloned.1.call-start
  9.7 0.7 all-gather.6.cloned.1.call-update
  10.4 0.0 reduce-scatter.2.cloned.1.call-start
  10.5 83.0 %all-gather.8.cloned.1.call-done = bf16[32,1,17536]{2,1,0:T(2,128)(2,1)} async-done(((bf16[1,1,17536]{2,1,0:T(2,128)(2,1)}), bf16[32,1,17536]{2,1,0:T(2,128)(2,1)}) %all-gather.8.cloned.1.call-update) | async-done | bytes 1122320 | tf_op jit(solution)/shard_map/all_gather | solution.py:17
  93.5 1.8 copy.53
  95.3 0.1 slice.8
  95.3 0.5 reshape_reshape.6
  95.9 1.2 reshape_reshape.7
  97.1 2.7 fusion.20
  99.8 94.4 %all-gather.6.cloned.1.call-done = bf16[1,2048,2048]{2,1,0:T(8,128)(2,1)} async-done(((bf16[1,64,2048]{2,1,0:T(8,128)(2,1)}), bf16[1,2048,2048]{2,1,0:T(8,128)(2,1)}) %all-gather.6.cloned.1.call-update) | async-done | bytes 8388624 | tf_op jit(solution)/shard_map/all_gather | solution.py:83
  194.3 9.0 %multiply_convert_fusion.1 = (bf16[512,2048]{0,1:T(8,128)(2,1)S(1)}, f32[512,2048]{0,1:T(8,128)S(1)}) fusion(bf16[1,2048,2048]{2,1,0:T(8,128)(2,1)} %all-gather.6.cloned.1.call-done, f32[2048,512]{1,0:T(8,128)} %fusion.20), kind=kOutput, calls=%fused_computation.17 | convolution fusion | flops 4305453056 | bytes 18874368 | tf_op jit(solution)/shard_map/dot_general | solution.py:84
  203.3 0.5 exponential_reduce_fusion
  203.8 0.6 multiply_reduce_fusion
  204.4 1.7 multiply_convert_fusion
  206.1 1.3 copy-done.10
  207.4 6.9 %convolution_convert_fusion = bf16[2048,2048]{1,0:T(8,128)(2,1)} fusion(bf16[512,2048]{0,1:T(8,128)(2,1)S(1)} %multiply_convert_fusion, f32[2048,512]{1,0:T(8,128)S(1)} %copy-done.1), kind=kOutput, calls=%fused_computation.4 | convolution fusion | flops 4304404480 | bytes 14680064 | tf_op jit(solution)/shard_map/dot_general | solution.py:60
  215.0 0.6 broadcast_in_dim.20
  215.6 5.5 %all-to-all-start.2 = ((f32[32,1,1]{2,1,0:T(1,128)}), f32[32,1,1]{2,1,0:T(1,128)S(1)}, u32[]{:S(2)}, u32[]{:S(2)}) async-start(f32[32,1,1]{2,1,0:T(1,128)} %broadcast_in_dim.20), calls=%async_computation.3 | async-start | bytes 32768 | tf_op jit(solution)/shard_map/all_to_all | solution.py:27
  221.1 0.6 convolution_convert_fusion.2
  221.8 0.2 reshape.54
  222.0 0.1 copy.54
  222.1 0.8 reshape.64
  222.8 8.0 %all-to-all-done.2 = f32[32,1,1]{2,1,0:T(1,128)S(1)} async-done(((f32[32,1,1]{2,1,0:T(1,128)}), f32[32,1,1]{2,1,0:T(1,128)S(1)}, u32[]{:S(2)}, u32[]{:S(2)}) %all-to-all-start.2) | async-done | bytes 160 | tf_op jit(solution)/shard_map/all_to_all | solution.py:27
  230.8 4.0 %all-to-all-start.1 = ((bf16[32,2,576]{2,1,0:T(2,128)(2,1)}), bf16[32,2,576]{2,1,0:T(2,128)(2,1)S(1)}, u32[]{:S(2)}, u32[]{:S(2)}) async-start(bf16[32,2,576]{2,1,0:T(2,128)(2,1)} %reshape.64), calls=%async_computation.2 | async-start | bytes 163840 | tf_op jit(solution)/shard_map/all_to_all | solution.py:44
  234.9 12.9 %fusion.14 = bf16[32,8,2048]{2,1,0:T(8,128)(2,1)} fusion(f32[2048,512]{1,0:T(8,128)} %fusion.20, bf16[512,2048]{0,1:T(8,128)(2,1)} %copy-done.10, bf16[1,2048,2048]{2,1,0:T(8,128)(2,1)} %all-gather.6.cloned.1.call-done, bf16[1,512,256]{2,1,0:T(8,128)(2,1)S(1)} %copy-done), kind=kOutput, calls=%fused_computation.20 | convolution fusion | flops 4841799680 | bytes 15990784 | tf_op jit(solution)/shard_map/dot_general | solution.py:60
  247.8 9.6 %all-to-all-start = ((bf16[32,8,2048]{2,1,0:T(8,128)(2,1)}), bf16[32,8,2048]{2,1,0:T(8,128)(2,1)S(1)}, u32[]{:S(2)}, u32[]{:S(2)}) async-start(bf16[32,8,2048]{2,1,0:T(8,128)(2,1)} %fusion.14), calls=%async_computation | async-start | bytes 2097152 | tf_op jit(solution)/shard_map/all_to_all | solution.py:44
  257.5 0.6 dynamic_slice.14
  258.7 0.6 fusion.27
  260.0 0.2 reshape.65
  260.2 0.1 convert_reduce_fusion.1
  260.3 1.6 collective-permute-start.2
  261.8 0.6 dynamic_slice.17
  264.4 0.6 reduce_sum.59
  265.0 1.1 collective-permute-done.2
  266.1 0.6 select_bitcast_fusion.2
  266.7 25.0 %all-to-all-done = bf16[32,8,2048]{2,1,0:T(8,128)(2,1)S(1)} async-done(((bf16[32,8,2048]{2,1,0:T(8,128)(2,1)}), bf16[32,8,2048]{2,1,0:T(8,128)(2,1)S(1)}, u32[]{:S(2)}, u32[]{:S(2)}) %all-to-all-start) | async-done | bytes 1048608 | tf_op jit(solution)/shard_map/all_to_all | solution.py:44
  291.7 0.2 convert_reduce_fusion
  291.9 1.6 collective-permute-start
  293.4 78.0 %reduce-scatter.2.cloned.1.call-done = bf16[64,2048]{1,0:T(8,128)(2,1)} async-done(((bf16[2048,2048]{1,0:T(8,128)(2,1)}), bf16[64,2048]{1,0:T(8,128)(2,1)}) %reduce-scatter.2.cloned.1.call-update) | async-done | bytes 262160 | tf_op jit(solution)/shard_map/reduce_scatter | solution.py:99
  371.5 1.0 fusion.18
  372.5 1.5 collective-permute-start.1
  374.0 0.6 select_bitcast_fusion.1
  374.6 6.5 %collective-permute-done.1 = bf16[64,2048]{1,0:T(8,128)(2,1)S(1)} collective-permute-done((bf16[64,2048]{1,0:T(8,128)(2,1)S(1)}, bf16[64,2048]{1,0:T(8,128)(2,1)S(1)}, u32[]{:S(2)}, u32[]{:S(2)}) %collective-permute-start.1) | collective-permute-done | bytes 262176 | tf_op jit(solution)/shard_map/ppermute | solution.py:51
  381.1 0.7 select_bitcast_fusion
  (32 shorter events, 0.2 us)
Async XLA Ops:
  7.2 90.0 %copy-start = (bf16[1,512,256]{2,1,0:T(8,128)(2,1)S(1)}, bf16[1,512,256]{2,1,0:T(8,128)(2,1)}, u32[]{:S(2)}) copy-start(bf16[1,512,256]{2,1,0:T(8,128)(2,1)} %param.9) | copy-start | bytes 786436
  7.2 86.3 %all-gather.8.cloned.1.call-start = ((), (), s32[]{:S(2)}) async-start(), calls=%async_computation.6 | async-start | bytes 2314752 | tf_op jit(solution)/shard_map/all_gather | solution.py:17
  9.7 184.6 %all-gather.6.cloned.1.call-start = ((), (), s32[]{:S(2)}) async-start(), calls=%async_computation.5 | async-start | bytes 8650752 | tf_op jit(solution)/shard_map/all_gather | solution.py:83
  10.4 361.1 %reduce-scatter.2.cloned.1.call-start = ((), (), s32[]{:S(2)}) async-start(), calls=%async_computation.4 | async-start | bytes 8650752 | tf_op jit(solution)/shard_map/reduce_scatter | solution.py:99
  99.8 103.9 %copy-start.5 = (s32[1,512]{1,0:T(1,128)S(1)}, s32[1,512]{1,0:T(1,128)}, u32[]{:S(2)}) copy-start(s32[1,512]{1,0:T(1,128)} %param.11) | copy-start | bytes 6148
  99.8 103.9 %copy-start.7 = (f32[1,512]{1,0:T(1,128)S(1)}, f32[1,512]{1,0:T(1,128)}, u32[]{:S(2)}) copy-start(f32[1,512]{1,0:T(1,128)} %param.10) | copy-start | bytes 6148
  204.4 3.0 copy-start.1
  206.1 1.3 copy-start.10
  215.6 15.2 %all-to-all-start.2 = ((f32[32,1,1]{2,1,0:T(1,128)}), f32[32,1,1]{2,1,0:T(1,128)S(1)}, u32[]{:S(2)}, u32[]{:S(2)}) async-start(f32[32,1,1]{2,1,0:T(1,128)} %broadcast_in_dim.20), calls=%async_computation.3 | async-start | bytes 32768 | tf_op jit(solution)/shard_map/all_to_all | solution.py:27
  230.8 17.0 %all-to-all-start.1 = ((bf16[32,2,576]{2,1,0:T(2,128)(2,1)}), bf16[32,2,576]{2,1,0:T(2,128)(2,1)S(1)}, u32[]{:S(2)}, u32[]{:S(2)}) async-start(bf16[32,2,576]{2,1,0:T(2,128)(2,1)} %reshape.64), calls=%async_computation.2 | async-start | bytes 163840 | tf_op jit(solution)/shard_map/all_to_all | solution.py:44
  234.9 22.6 %copy-start.8 = (s32[8]{0:T(128)S(1)}, s32[8]{0:T(128)}, u32[]{:S(2)}) copy-start(s32[8]{0:T(128)} %param.16) | copy-start | bytes 100
  234.9 23.8 %copy-start.6 = (f32[8]{0:T(128)S(1)}, f32[8]{0:T(128)}, u32[]{:S(2)}) copy-start(f32[8]{0:T(128)} %param.15) | copy-start | bytes 100
  234.9 25.4 %copy-start.4 = (bf16[1,64,18]{1,2,0:T(8,128)(2,1)S(1)}, bf16[1,64,18]{1,2,0:T(8,128)(2,1)}, u32[]{:S(2)}) copy-start(bf16[1,64,18]{1,2,0:T(8,128)(2,1)} %param.14) | copy-start | bytes 6916
  234.9 26.9 %copy-start.9 = (s32[8]{0:T(128)S(1)}, s32[8]{0:T(128)}, u32[]{:S(2)}) copy-start(s32[8]{0:T(128)} %param.17) | copy-start | bytes 100
  234.9 56.9 %copy-start.3 = (bf16[1,8,2048]{2,1,0:T(8,128)(2,1)S(1)}, bf16[1,8,2048]{2,1,0:T(8,128)(2,1)}, u32[]{:S(2)}) copy-start(bf16[1,8,2048]{2,1,0:T(8,128)(2,1)} %param.12) | copy-start | bytes 98308
  234.9 136.6 %copy-start.2 = (bf16[1,64,2048]{2,1,0:T(8,128)(2,1)S(1)}, bf16[1,64,2048]{2,1,0:T(8,128)(2,1)}, u32[]{:S(2)}) copy-start(bf16[1,64,2048]{2,1,0:T(8,128)(2,1)} %param.13) | copy-start | bytes 786436
  247.8 43.8 %all-to-all-start = ((bf16[32,8,2048]{2,1,0:T(8,128)(2,1)}), bf16[32,8,2048]{2,1,0:T(8,128)(2,1)S(1)}, u32[]{:S(2)}, u32[]{:S(2)}) async-start(bf16[32,8,2048]{2,1,0:T(8,128)(2,1)} %fusion.14), calls=%async_computation | async-start | bytes 2097152 | tf_op jit(solution)/shard_map/all_to_all | solution.py:44
  260.3 5.9 %collective-permute-start.2 = (bf16[64,18]{0,1:T(8,128)(2,1)S(1)}, bf16[64,18]{0,1:T(8,128)(2,1)S(1)}, u32[]{:S(2)}, u32[]{:S(2)}) collective-permute-start(bf16[64,18]{0,1:T(8,128)(2,1)S(1)} %fusion.23), channel_id=1, source_target_pairs={{224,0},{0,32},{32,64},{64,96},{96,128},{128,160},{160,192},{192,2... | collective-permute-start | bytes 6920 | tf_op jit(solution)/shard_map/ppermute | solution.py:51
  291.9 82.1 %collective-permute-start = (bf16[8,2048]{1,0:T(8,128)(2,1)S(1)}, bf16[8,2048]{1,0:T(8,128)(2,1)S(1)}, u32[]{:S(2)}, u32[]{:S(2)}) collective-permute-start(bf16[8,2048]{1,0:T(8,128)(2,1)S(1)} %fusion.22), channel_id=1, source_target_pairs={{224,0},{0,32},{32,64},{64,96},{96,128},{128,160},{160,192},{192,2... | collective-permute-start | bytes 98312 | tf_op jit(solution)/shard_map/ppermute | solution.py:51
  372.5 8.6 %collective-permute-start.1 = (bf16[64,2048]{1,0:T(8,128)(2,1)S(1)}, bf16[64,2048]{1,0:T(8,128)(2,1)S(1)}, u32[]{:S(2)}, u32[]{:S(2)}) collective-permute-start(bf16[64,2048]{1,0:T(8,128)(2,1)S(1)} %fusion.18), channel_id=1, source_target_pairs={{224,0},{0,32},{32,64},{64,96},{96,128},{128,160},{160,192},{192,2... | collective-permute-start | bytes 786440 | tf_op jit(solution)/shard_map/ppermute | solution.py:51
Sparse Core Ops, SparseCore 0:
  11.3 82.1 all-gather.7
  96.3 97.9 all-gather.5
  214.5 156.9 reduce-scatter.1
where the time goes:
time: 390 us; the launch traced here: 389 us
  waiting for transfers between devices  297 us (76%)
  matrix products  34.3 us (9%)
  starting transfers between devices  23.8 us (6%)
  between operations  19.1 us (5%)
  local copies, waits for them, and re-layouts  11 us (3%)
  other arithmetic  4.48 us (1%)
    all_gather x1, waiting for transfers between devices, local(): whole = lax.all_gather(own_middle, 'dp', axis=0, tiled=True)  94.4 us
    all_gather x1, waiting for transfers between devices, gather_packed(): lines, at, done = (lax.all_gather(line, axis), 0, [])  83 us
    reduce_scatter x1, waiting for transfers between devices, local(): lax.psum_scatter(contract_rows(hidden1, grad_pre2).astype(jnp.bfloat16),...  78 us
    all_to_all x2, waiting for transfers between devices, sum_at_owner(): parts = lax.all_to_all(in_blocks(shard, dim, peers), axis, 0, 0, tiled=True)  25 us
    dot_general x3, matrix products, contract_rows(): lax.dot_general(left, right, (((0,), (0,)), ((), ())), preferred_element_...  20.5 us
    all_to_all x2, starting transfers between devices, sum_at_owner(): parts = lax.all_to_all(in_blocks(shard, dim, peers), axis, 0, 0, tiled=True)  13.6 us
    dot_general x1, matrix products, local(): pre2 = jnp.dot(hidden1, whole, preferred_element_type=jnp.float32)  8.98 us
    all_to_all x1, waiting for transfers between devices, from_everyone(): lax.all_to_all(jnp.broadcast_to(shard[None], (peers, *shard.shape)), axis...  7.97 us
  transfers between devices with their start and end apart: 9, of which 7 were waited for; matrix products, arithmetic and copies ran while one was open for 7% of the time, Pallas kernels for 0%

commit v1 on v0

--- a/solution.py
+++ b/solution.py
@@ -80,7 +80,10 @@
     first, head = gather_packed((own_first, own_head), "dp", (0, 0))
     pre1 = jnp.dot(obs, first, preferred_element_type=jnp.float32)
     hidden1 = jax.nn.silu(pre1).astype(jnp.bfloat16)
-    whole = lax.all_gather(own_middle, "dp", axis=0, tiled=True)
+    size = lax.axis_size("dp")
+    shards = jnp.stack([own_middle for _ in range(size)])
+    shards = lax.all_to_all(shards, "dp", split_axis=0, concat_axis=0)
+    whole = jnp.concatenate(shards, axis=0)
     pre2 = jnp.dot(hidden1, whole, preferred_element_type=jnp.float32)
     hidden2 = jax.nn.silu(pre2).astype(jnp.bfloat16)
     squash = jnp.tanh(jnp.dot(hidden2, head, preferred_element_type=jnp.float32) / CAP)

time: 390 us -> 414 us (1.062)
  starting transfers between devices: 23.8 us -> 34.3 us
  waiting for transfers between devices: 297 us -> 306 us
    all_gather x1 -> x0, waiting for transfers between devices: 94.4 us -> none  [local(): whole = lax.all_gather(own_middle, 'dp', axis=0, tiled=True)]
    all_to_all x0 -> x1, waiting for transfers between devices: none -> 82.9 us  [local(): shards = lax.all_to_all(shards, 'dp', split_axis=0, concat_axis=0)]
    all_gather x1, waiting for transfers between devices: 83 us -> 104 us  [gather_packed(): lines, at, done = (lax.all_gather(line, axis), 0, [])]
    all_to_all x0 -> x1, starting transfers between devices: none -> 10.7 us  [local(): shards = lax.all_to_all(shards, 'dp', split_axis=0, concat_axis=0)]
    another operation x0 -> x1, local copies, waits for them, and re-layouts: none -> 5.29 us  [local(): shards = jnp.stack([own_middle for _ in range(size)])]
where the time goes in v1:
time: 414 us; the launch traced here: 413 us
  waiting for transfers between devices  306 us (74%)
  starting transfers between devices  34.3 us (8%)
  matrix products  34.3 us (8%)
  between operations  19.4 us (5%)
  local copies, waits for them, and re-layouts  14.8 us (4%)
  other arithmetic  4.48 us (1%)
    all_gather x1, waiting for transfers between devices, gather_packed(): lines, at, done = (lax.all_gather(line, axis), 0, [])  104 us
    all_to_all x1, waiting for transfers between devices, local(): shards = lax.all_to_all(shards, 'dp', split_axis=0, concat_axis=0)  82.9 us
    reduce_scatter x1, waiting for transfers between devices, local(): lax.psum_scatter(contract_rows(hidden1, grad_pre2).astype(jnp.bfloat16),...  78.6 us
    all_to_all x2, waiting for transfers between devices, sum_at_owner(): parts = lax.all_to_all(in_blocks(shard, dim, peers), axis, 0, 0, tiled=True)  24.9 us
    dot_general x3, matrix products, contract_rows(): lax.dot_general(left, right, (((0,), (0,)), ((), ())), preferred_element_...  20.5 us
    all_to_all x2, starting transfers between devices, sum_at_owner(): parts = lax.all_to_all(in_blocks(shard, dim, peers), axis, 0, 0, tiled=True)  13.8 us
    all_to_all x1, starting transfers between devices, local(): shards = lax.all_to_all(shards, 'dp', split_axis=0, concat_axis=0)  10.7 us
    dot_general x1, matrix products, local(): pre2 = jnp.dot(hidden1, whole, preferred_element_type=jnp.float32)  9 us
  transfers between devices with their start and end apart: 9, of which 7 were waited for; matrix products, arithmetic and copies ran while one was open for 7% of the time, Pallas kernels for 0%

profile of v1, /device:TPU:2, one launch (start us, length us, event | category | flops | bytes accessed | tf_op | source)
XLA Modules:
  0.0 413.4 jit_solution(4473134936704079647)
XLA Ops:
  7.2 5.3 %stack.3 = bf16[32,64,2048]{2,1,0:T(8,128)(2,1)} broadcast(bf16[64,2048]{1,0:T(8,128)(2,1)} %bitcast.82), dimensions={1,2} | broadcast | bytes 8650752 | tf_op jit(solution)/shard_map/stack | solution.py:84
  12.5 10.7 %all-to-all-start = ((bf16[32,64,2048]{2,1,0:T(8,128)(2,1)}), bf16[32,64,2048]{2,1,0:T(8,128)(2,1)}, u32[]{:S(2)}, u32[]{:S(2)}) async-start(bf16[32,64,2048]{2,1,0:T(8,128)(2,1)} %stack.3), calls=%async_computation | async-start | bytes 16777216 | tf_op jit(solution)/shard_map/all_to_all | solution.py:85
  23.2 0.0 all-gather.4.cloned.1.call-start
  23.2 0.1 copy.37
  23.3 0.1 reshape_squeeze.7
  23.5 0.7 reshape.64
  24.2 0.0 reduce-scatter.2.cloned.1.call-start
  24.3 104.2 %all-gather.4.cloned.1.call-done = bf16[32,1,17536]{2,1,0:T(2,128)(2,1)} async-done(((bf16[1,1,17536]{2,1,0:T(2,128)(2,1)}), bf16[32,1,17536]{2,1,0:T(2,128)(2,1)}) %all-gather.4.cloned.1.call-update) | async-done | bytes 1122320 | tf_op jit(solution)/shard_map/all_gather | solution.py:17
  128.5 1.8 copy.53
  130.2 0.1 slice.8
  130.3 0.5 reshape_reshape.6
  130.9 1.2 reshape_reshape.7
  132.1 2.7 fusion.11
  134.8 82.9 %all-to-all-done = bf16[32,64,2048]{2,1,0:T(8,128)(2,1)} async-done(((bf16[32,64,2048]{2,1,0:T(8,128)(2,1)}), bf16[32,64,2048]{2,1,0:T(8,128)(2,1)}, u32[]{:S(2)}, u32[]{:S(2)}) %all-to-all-start) | async-done | bytes 8388640 | tf_op jit(solution)/shard_map/all_to_all | solution.py:85
  217.8 9.0 %multiply_convert_fusion.1 = (bf16[512,2048]{0,1:T(8,128)(2,1)S(1)}, f32[512,2048]{0,1:T(8,128)S(1)}) fusion(bf16[2048,2048]{1,0:T(8,128)(2,1)} %bitcast.8, f32[2048,512]{1,0:T(8,128)} %fusion.11), kind=kOutput, calls=%fused_computation.13 | convolution fusion | flops 4305453056 | bytes 18874368 | tf_op jit(solution)/shard_map/dot_general | solution.py:87
  226.8 0.5 exponential_reduce_fusion
  227.3 0.6 multiply_reduce_fusion
  227.9 1.7 multiply_convert_fusion
  229.6 1.3 copy-done.10
  230.9 6.9 %convolution_convert_fusion = bf16[2048,2048]{1,0:T(8,128)(2,1)} fusion(bf16[512,2048]{0,1:T(8,128)(2,1)S(1)} %multiply_convert_fusion, f32[2048,512]{1,0:T(8,128)S(1)} %copy-done.1), kind=kOutput, calls=%fused_computation | convolution fusion | flops 4304404480 | bytes 14680064 | tf_op jit(solution)/shard_map/dot_general | solution.py:60
  238.5 0.6 broadcast_in_dim.20
  239.1 4.9 %all-to-all-start.3 = ((f32[32,1,1]{2,1,0:T(1,128)}), f32[32,1,1]{2,1,0:T(1,128)S(1)}, u32[]{:S(2)}, u32[]{:S(2)}) async-start(f32[32,1,1]{2,1,0:T(1,128)} %broadcast_in_dim.20), calls=%async_computation.4 | async-start | bytes 32768 | tf_op jit(solution)/shard_map/all_to_all | solution.py:27
  244.0 0.6 convolution_convert_fusion.2
  244.6 0.2 reshape.59
  244.8 0.1 copy.54
  244.9 0.8 reshape.67
  245.7 8.0 %all-to-all-done.3 = f32[32,1,1]{2,1,0:T(1,128)S(1)} async-done(((f32[32,1,1]{2,1,0:T(1,128)}), f32[32,1,1]{2,1,0:T(1,128)S(1)}, u32[]{:S(2)}, u32[]{:S(2)}) %all-to-all-start.3) | async-done | bytes 160 | tf_op jit(solution)/shard_map/all_to_all | solution.py:27
  253.7 4.0 all-to-all-start.2
  257.8 12.9 %fusion.8 = bf16[32,8,2048]{2,1,0:T(8,128)(2,1)} fusion(f32[2048,512]{1,0:T(8,128)} %fusion.11, bf16[2048,2048]{1,0:T(8,128)(2,1)} %bitcast.8, bf16[512,2048]{0,1:T(8,128)(2,1)} %copy-done.10, bf16[1,512,256]{2,1,0:T(8,128)(2,1)S(1)} %copy-done), kind=kOutput, calls=%fused_computation.16 | convolution fusion | flops 4841799680 | bytes 15990784 | tf_op jit(solution)/shard_map/dot_general | solution.py:60
  270.7 9.8 %all-to-all-start.1 = ((bf16[32,8,2048]{2,1,0:T(8,128)(2,1)}), bf16[32,8,2048]{2,1,0:T(8,128)(2,1)S(1)}, u32[]{:S(2)}, u32[]{:S(2)}) async-start(bf16[32,8,2048]{2,1,0:T(8,128)(2,1)} %fusion.8), calls=%async_computation.1 | async-start | bytes 2097152 | tf_op jit(solution)/shard_map/all_to_all | solution.py:44
  280.5 0.6 dynamic_slice.14
  281.7 0.6 fusion.19
  283.0 0.2 reshape.68
  283.2 0.1 convert_reduce_fusion.1
  283.3 1.6 collective-permute-start.2
  284.9 0.6 dynamic_slice.17
  287.4 0.6 reduce_sum.59
  288.1 1.0 collective-permute-done.2
  289.1 0.6 select_bitcast_fusion.2
  289.7 24.9 %all-to-all-done.1 = bf16[32,8,2048]{2,1,0:T(8,128)(2,1)S(1)} async-done(((bf16[32,8,2048]{2,1,0:T(8,128)(2,1)}), bf16[32,8,2048]{2,1,0:T(8,128)(2,1)S(1)}, u32[]{:S(2)}, u32[]{:S(2)}) %all-to-all-start.1) | async-done | bytes 1048608 | tf_op jit(solution)/shard_map/all_to_all | solution.py:44
  314.6 0.2 convert_reduce_fusion
  314.8 1.7 collective-permute-start
  316.5 78.6 %reduce-scatter.2.cloned.1.call-done = bf16[64,2048]{1,0:T(8,128)(2,1)} async-done(((bf16[2048,2048]{1,0:T(8,128)(2,1)}), bf16[64,2048]{1,0:T(8,128)(2,1)}) %reduce-scatter.2.cloned.1.call-update) | async-done | bytes 262160 | tf_op jit(solution)/shard_map/reduce_scatter | solution.py:102
  395.1 1.0 subtract_convert_fusion
  396.1 1.5 collective-permute-start.1
  397.6 0.6 select_bitcast_fusion.1
  398.2 6.4 %collective-permute-done.1 = bf16[64,2048]{1,0:T(8,128)(2,1)S(1)} collective-permute-done((bf16[64,2048]{1,0:T(8,128)(2,1)S(1)}, bf16[64,2048]{1,0:T(8,128)(2,1)S(1)}, u32[]{:S(2)}, u32[]{:S(2)}) %collective-permute-start.1) | collective-permute-done | bytes 262176 | tf_op jit(solution)/shard_map/ppermute | solution.py:51
  404.7 0.7 select_bitcast_fusion
  (32 shorter events, 0.2 us)
Async XLA Ops:
  7.2 124.9 %copy-start = (bf16[1,512,256]{2,1,0:T(8,128)(2,1)S(1)}, bf16[1,512,256]{2,1,0:T(8,128)(2,1)}, u32[]{:S(2)}) copy-start(bf16[1,512,256]{2,1,0:T(8,128)(2,1)} %param.9) | copy-start | bytes 786436
  12.5 10.7 %copy-start.4 = (bf16[1,64,18]{1,2,0:T(8,128)(2,1)S(1)}, bf16[1,64,18]{1,2,0:T(8,128)(2,1)}, u32[]{:S(2)}) copy-start(bf16[1,64,18]{1,2,0:T(8,128)(2,1)} %param.14) | copy-start | bytes 6916
  12.5 11.0 %copy-start.3 = (bf16[1,8,2048]{2,1,0:T(8,128)(2,1)S(1)}, bf16[1,8,2048]{2,1,0:T(8,128)(2,1)}, u32[]{:S(2)}) copy-start(bf16[1,8,2048]{2,1,0:T(8,128)(2,1)} %param.12) | copy-start | bytes 98308
  12.5 205.3 %all-to-all-start = ((bf16[32,64,2048]{2,1,0:T(8,128)(2,1)}), bf16[32,64,2048]{2,1,0:T(8,128)(2,1)}, u32[]{:S(2)}, u32[]{:S(2)}) async-start(bf16[32,64,2048]{2,1,0:T(8,128)(2,1)} %stack.3), calls=%async_computation | async-start | bytes 16777216 | tf_op jit(solution)/shard_map/all_to_all | solution.py:85
  23.2 105.3 %all-gather.4.cloned.1.call-start = ((), (), s32[]{:S(2)}) async-start(), calls=%async_computation.6 | async-start | bytes 2314752 | tf_op jit(solution)/shard_map/all_gather | solution.py:17
  24.2 370.9 %reduce-scatter.2.cloned.1.call-start = ((), (), s32[]{:S(2)}) async-start(), calls=%async_computation.5 | async-start | bytes 8650752 | tf_op jit(solution)/shard_map/reduce_scatter | solution.py:102
  217.8 9.5 %copy-start.5 = (s32[1,512]{1,0:T(1,128)S(1)}, s32[1,512]{1,0:T(1,128)}, u32[]{:S(2)}) copy-start(s32[1,512]{1,0:T(1,128)} %param.11) | copy-start | bytes 6148
  217.8 9.5 %copy-start.7 = (f32[1,512]{1,0:T(1,128)S(1)}, f32[1,512]{1,0:T(1,128)}, u32[]{:S(2)}) copy-start(f32[1,512]{1,0:T(1,128)} %param.10) | copy-start | bytes 6148
  227.9 3.0 copy-start.1
  229.6 1.3 copy-start.10
  239.1 14.5 %all-to-all-start.3 = ((f32[32,1,1]{2,1,0:T(1,128)}), f32[32,1,1]{2,1,0:T(1,128)S(1)}, u32[]{:S(2)}, u32[]{:S(2)}) async-start(f32[32,1,1]{2,1,0:T(1,128)} %broadcast_in_dim.20), calls=%async_computation.4 | async-start | bytes 32768 | tf_op jit(solution)/shard_map/all_to_all | solution.py:27
  253.7 17.0 %all-to-all-start.2 = ((bf16[32,2,576]{2,1,0:T(2,128)(2,1)}), bf16[32,2,576]{2,1,0:T(2,128)(2,1)S(1)}, u32[]{:S(2)}, u32[]{:S(2)}) async-start(bf16[32,2,576]{2,1,0:T(2,128)(2,1)} %reshape.67), calls=%async_computation.3 | async-start | bytes 163840 | tf_op jit(solution)/shard_map/all_to_all | solution.py:44
  257.7 22.8 %copy-start.8 = (s32[8]{0:T(128)S(1)}, s32[8]{0:T(128)}, u32[]{:S(2)}) copy-start(s32[8]{0:T(128)} %param.16) | copy-start | bytes 100
  257.7 24.0 %copy-start.6 = (f32[8]{0:T(128)S(1)}, f32[8]{0:T(128)}, u32[]{:S(2)}) copy-start(f32[8]{0:T(128)} %param.15) | copy-start | bytes 100
  257.7 27.2 %copy-start.9 = (s32[8]{0:T(128)S(1)}, s32[8]{0:T(128)}, u32[]{:S(2)}) copy-start(s32[8]{0:T(128)} %param.17) | copy-start | bytes 100
  257.7 137.3 %copy-start.2 = (bf16[1,64,2048]{2,1,0:T(8,128)(2,1)S(1)}, bf16[1,64,2048]{2,1,0:T(8,128)(2,1)}, u32[]{:S(2)}) copy-start(bf16[1,64,2048]{2,1,0:T(8,128)(2,1)} %param.13) | copy-start | bytes 786436
  270.7 44.0 %all-to-all-start.1 = ((bf16[32,8,2048]{2,1,0:T(8,128)(2,1)}), bf16[32,8,2048]{2,1,0:T(8,128)(2,1)S(1)}, u32[]{:S(2)}, u32[]{:S(2)}) async-start(bf16[32,8,2048]{2,1,0:T(8,128)(2,1)} %fusion.8), calls=%async_computation.1 | async-start | bytes 2097152 | tf_op jit(solution)/shard_map/all_to_all | solution.py:44
  283.3 5.8 %collective-permute-start.2 = (bf16[64,18]{0,1:T(8,128)(2,1)S(1)}, bf16[64,18]{0,1:T(8,128)(2,1)S(1)}, u32[]{:S(2)}, u32[]{:S(2)}) collective-permute-start(bf16[64,18]{0,1:T(8,128)(2,1)S(1)} %fusion.14), channel_id=1, source_target_pairs={{224,0},{0,32},{32,64},{64,96},{96,128},{128,160},{160,192},{192,2... | collective-permute-start | bytes 6920 | tf_op jit(solution)/shard_map/ppermute | solution.py:51
  314.8 82.8 %collective-permute-start = (bf16[8,2048]{1,0:T(8,128)(2,1)S(1)}, bf16[8,2048]{1,0:T(8,128)(2,1)S(1)}, u32[]{:S(2)}, u32[]{:S(2)}) collective-permute-start(bf16[8,2048]{1,0:T(8,128)(2,1)S(1)} %fusion.13), channel_id=1, source_target_pairs={{224,0},{0,32},{32,64},{64,96},{96,128},{128,160},{160,192},{192,2... | collective-permute-start | bytes 98312 | tf_op jit(solution)/shard_map/ppermute | solution.py:51
  396.1 8.6 %collective-permute-start.1 = (bf16[64,2048]{1,0:T(8,128)(2,1)S(1)}, bf16[64,2048]{1,0:T(8,128)(2,1)S(1)}, u32[]{:S(2)}, u32[]{:S(2)}) collective-permute-start(bf16[64,2048]{1,0:T(8,128)(2,1)S(1)} %subtract_convert_fusion), channel_id=1, source_target_pairs={{224,0},{0,32},{32,64},{64,96},{96,128},{128,160},{160,192},{192,2... | collective-permute-start | bytes 786440 | tf_op jit(solution)/shard_map/ppermute | solution.py:51
Sparse Core Ops, SparseCore 0:
  27.3 101.1 all-gather.3
  238.0 157.0 reduce-scatter.1
